TPU v7x, 32 devices: a whole 2x2x4 slice. The times are simulated.
32 devices in a mesh: dom: 32 (over z, y, x, core).
Axes of the slice: x: 2, y: 2, z: 4, core: 2. Of those that a mesh axis runs over, the one named last changes fastest.
Arguments:
- concentration: float32 [1024, 128], P('dom'), may hold values from 0 to 1
- reaction_rate: float32 [1024, 128], P('dom'), may hold values from 0.5 to 4
- step_size: float32 [1], replicated, may hold values from 1 to 2
- block_values: float32 [1024, 5, 128, 128], P('dom'), may hold values from -40 to 48, as said below
- block_columns: int32 [1024, 5], P('dom'), may hold values from 0 to 95, as said below
- row_lengths: int32 [1024], P('dom'), may hold values from 2 to 5, as said below
- send_lists: int32 [32, 4, 16], P('dom'), may hold values from 0 to 31, as said below
Outputs:
- next_concentration: float32 [1024, 128], P('dom')
Inputs may be any that keep to these rules, and one draw needn't show every extreme that they name: `send_lists`: for every partition and offset index q (offsets -2, -1, +1, +2), 16 distinct local block indices. `block_columns`: slot 0 of a block row is the row's own local block; live slots name a local block (below 32) or a ghost slot 32 + q * 16 + g of a block that the partition at offset index q sends; slot 1 of local block row q, for q = 0..3, is a ghost slot of offset index q; slots at or past the row's length repeat the row's own local block. `row_lengths`: some block row has all 5 slots live. `block_values`: slot 0 of every block row holds 8 times the identity plus a full random block; the other slots hold full random blocks.
All inputs are finite; a program needn't handle non-finite values.
Results may differ from a plain program's by a relative error of at most 0.00016.
Values sent between devices are 32-bit elements; how exact they have to be, the bound alone decides.
A program may use at most 64 MiB of HBM per device.

v0:
```python
import jax
import jax.numpy as jnp
from jax import lax
from jax.sharding import PartitionSpec as P

KRYLOV = 3
RESTARTS = 2


epsilon = 1e-06


def passed_along(value, axis, by):
    length = lax.axis_size(axis)
    return lax.ppermute(value, axis, [(i, (i + by) % length) for i in range(length)])


def extend_field(field, send_lists):
    packets = field[send_lists[0]]
    from_minus_two = passed_along(packets[0], "dom", -2)
    from_minus_one = passed_along(packets[1], "dom", -1)
    from_plus_one = passed_along(packets[2], "dom", 1)
    from_plus_two = passed_along(packets[3], "dom", 2)
    ghosts = [from_minus_two, from_minus_one, from_plus_one, from_plus_two]
    return jnp.concatenate([field] + ghosts, axis=0)


def product(block_values, block_columns, active, send_lists, field):
    extended = extend_field(field, send_lists)
    gathered = extended[block_columns] * active[:, :, None]
    return jnp.einsum("bsij,bsj->bi", block_values, gathered, precision=lax.Precision.HIGHEST)


def phi_column(hessenberg, substep):
    order = hessenberg.shape[0]
    augmented = jnp.zeros((order + 1, order + 1), jnp.float32)
    augmented = augmented.at[:order, :order].set(substep * hessenberg).at[0, order].set(1.0)
    reduced = augmented / 64.0
    identity = jnp.eye(order + 1, dtype=jnp.float32)
    series = identity
    for degree in range(12, 0, -1):
        series = identity + jnp.dot(reduced, series, precision=lax.Precision.HIGHEST) / degree
    for square_turn in range(6):
        series = jnp.dot(series, series, precision=lax.Precision.HIGHEST)
    return series[:order, order]


def local_dots(vectors, mapped):
    return jnp.einsum("kbi,bi->k", vectors, mapped, precision=lax.Precision.HIGHEST)


def combine(weights, vectors):
    return jnp.einsum("k,kbi->bi", weights, vectors, precision=lax.Precision.HIGHEST)


def krylov(start, apply):
    squared = lax.psum(jnp.sum(start * start), "dom")
    magnitude = jnp.sqrt(squared + epsilon)
    vectors = jnp.zeros((KRYLOV,) + start.shape, jnp.float32).at[0].set(start / magnitude)
    hessenberg = jnp.zeros((KRYLOV, KRYLOV), jnp.float32)
    mapped = apply(vectors[0])
    projection = lax.psum(local_dots(vectors, mapped), "dom")
    residue = mapped - combine(projection, vectors)
    hessenberg = hessenberg.at[:, 0].set(projection)
    for column in range(1, KRYLOV):
        mapped = apply(residue)
        inner, self_term, residue_square = lax.psum(
            (local_dots(vectors, mapped), jnp.sum(residue * mapped), jnp.sum(residue * residue)),
            "dom",
        )
        length = jnp.sqrt(residue_square + epsilon)
        vectors = vectors.at[column].set(residue / length)
        projection = (inner / length).at[column].set(self_term / (length * length))
        hessenberg = hessenberg.at[column, column - 1].set(length).at[:, column].set(projection)
        residue = mapped / length - combine(projection, vectors)
    return (magnitude, vectors, hessenberg)


def shards(
    concentration, reaction_rate, step_size, block_values, block_columns, row_lengths, send_lists
):
    slot_count = block_columns.shape[1]
    active = (jnp.arange(slot_count, dtype=jnp.int32)[None, :] < row_lengths[:, None]).astype(
        jnp.float32
    )
    slope = reaction_rate * (1.0 - 2.0 * concentration)

    def operator(field):
        return product(block_values, block_columns, active, send_lists, field)

    def apply(field):
        return slope * field - operator(field)

    forcing = reaction_rate * concentration * (1.0 - concentration) - operator(concentration)
    substep = step_size[0] / RESTARTS
    increment = jnp.zeros_like(concentration)
    for restart in range(RESTARTS):
        start = forcing if restart == 0 else apply(increment) + forcing
        magnitude, vectors, hessenberg = krylov(start, apply)
        weights = phi_column(hessenberg, substep)
        increment = increment + substep * magnitude * combine(weights, vectors)
    return concentration + increment


def solution(mesh):
    placed = (
        P("dom", None),
        P("dom", None),
        P(),
        P("dom", None, None, None),
        P("dom", None),
        P("dom"),
        P("dom", None, None),
    )
    return jax.shard_map(
        shards, mesh=mesh, in_specs=placed, out_specs=P("dom", None), check_vma=False
    )
```

profile of v0, /device:TPU:12, one launch (start us, length us, event | category | flops | bytes accessed | tf_op | source)
XLA Modules:
  0.0 542.9 jit_solution(12244045466587664961)
XLA Ops:
  2.1 1.5 collective-permute-start
  9.5 12.6 %fusion.36 = f32[32,1,128,1]{2,1,3,0:T(1,128)S(1)} fusion(f32[32,5,128,128]{3,2,1,0:T(8,128)} %param.58, f32[32,5,128,1]{2,1,0,3:T(8,128)S(1)} %multiply_bitcast_fusion.7), kind=kOutput, calls=%fused_computation.132 | convolution fusion | flops 31457280 | bytes 10584064 | tf_op jit(solution)/shard_map/bsij,bsj->bi/dot_general | solution.py:31
  22.7 46.0 %psum.112 = f32[]{:T(128)} all-reduce(f32[]{:T(128)} %get-tuple-element.335), channel_id=1, replica_groups=mesh['dom'=32] {'dom'}, use_global_device_ids=true, to_apply=%region_1.0 | all-reduce | flops 1 | bytes 8 | tf_op jit(solution)/shard_map/psum | solution.py:57
  75.5 2.6 collective-permute-done.6
  79.9 12.6 %fusion.34 = f32[32,1,128,1]{2,1,3,0:T(1,128)S(1)} fusion(f32[32,5,128,128]{3,2,1,0:T(8,128)} %param.58, f32[32,5,128,1]{2,1,0,3:T(8,128)S(1)} %multiply_bitcast_fusion.6), kind=kOutput, calls=%fused_computation.130 | convolution fusion | flops 31457280 | bytes 10584064 | tf_op jit(solution)/shard_map/bsij,bsj->bi/dot_general | solution.py:31
  93.0 41.7 %psum.113 = f32[3]{0:T(128)S(1)} all-reduce(f32[3]{0:T(128)S(1)} %convolution_bitcast_fusion.7), channel_id=1, replica_groups=mesh['dom'=32] {'dom'}, use_global_device_ids=true, to_apply=%region_3.0 | all-reduce | flops 3 | bytes 24 | tf_op jit(solution)/shard_map/psum | solution.py:62
  135.6 1.5 collective-permute-start.8
  139.3 2.3 collective-permute-done.10
  143.4 12.6 %fusion.32 = f32[32,1,128,1]{2,1,3,0:T(1,128)S(1)} fusion(f32[32,5,128,128]{3,2,1,0:T(8,128)} %param.58, f32[32,5,128,1]{2,1,0,3:T(8,128)S(1)} %multiply_bitcast_fusion.5), kind=kOutput, calls=%fused_computation.128 | convolution fusion | flops 31457280 | bytes 10584064 | tf_op jit(solution)/shard_map/bsij,bsj->bi/dot_general | solution.py:31
  157.1 42.4 %all-reduce.9 = (f32[]{:T(128)}, f32[3]{0:T(128)S(1)}, f32[]{:T(128)}) all-reduce(f32[]{:T(128)} %get-tuple-element.300, f32[3]{0:T(128)S(1)} %convolution_bitcast_fusion.6, f32[]{:T(128)} %get-tuple-element.299), channel_id=1, replica_groups=mesh['dom'=32] {'dom'}, use_global_device_ids=true, to_apply=%region_5.0 | all-reduce | flops 5 | bytes 40 | tf_op jit(solution)/shard_map/psum | solution.py:67
  201.7 1.3 collective-permute-start.12
  205.4 1.6 collective-permute-done.14
  208.9 12.6 %fusion.30 = f32[32,1,128,1]{2,1,3,0:T(1,128)S(1)} fusion(f32[32,5,128,128]{3,2,1,0:T(8,128)} %param.58, f32[32,5,128,1]{2,1,0,3:T(8,128)S(1)} %multiply_bitcast_fusion.4), kind=kOutput, calls=%fused_computation.126 | convolution fusion | flops 31457280 | bytes 10584064 | tf_op jit(solution)/shard_map/bsij,bsj->bi/dot_general | solution.py:31
  222.6 42.4 %all-reduce.8 = (f32[]{:T(128)}, f32[3]{0:T(128)S(1)}, f32[]{:T(128)}) all-reduce(f32[]{:T(128)} %get-tuple-element.298, f32[3]{0:T(128)S(1)} %convolution_bitcast_fusion.5, f32[]{:T(128)} %get-tuple-element.297), channel_id=1, replica_groups=mesh['dom'=32] {'dom'}, use_global_device_ids=true, to_apply=%region_11.0 | all-reduce | flops 5 | bytes 40 | tf_op jit(solution)/shard_map/psum | solution.py:67
  266.7 2.5 fusion.76
  269.2 1.9 scatter.96
  279.1 1.6 collective-permute-done.18
  282.6 12.6 %fusion.28 = f32[32,1,128,1]{2,1,3,0:T(1,128)S(1)} fusion(f32[32,5,128,128]{3,2,1,0:T(8,128)} %param.58, f32[32,5,128,1]{2,1,0,3:T(8,128)S(1)} %multiply_bitcast_fusion.3), kind=kOutput, calls=%fused_computation.124 | convolution fusion | flops 31457280 | bytes 10584064 | tf_op jit(solution)/shard_map/bsij,bsj->bi/dot_general | solution.py:31
  295.9 42.2 %psum.120 = f32[]{:T(128)} all-reduce(f32[]{:T(128)} %get-tuple-element.321), channel_id=1, replica_groups=mesh['dom'=32] {'dom'}, use_global_device_ids=true, to_apply=%region_17.0 | all-reduce | flops 1 | bytes 8 | tf_op jit(solution)/shard_map/psum | solution.py:57
  339.3 1.3 collective-permute-start.20
  343.1 1.6 collective-permute-done.22
  346.5 12.6 %fusion.26 = f32[32,1,128,1]{2,1,3,0:T(1,128)S(1)} fusion(f32[32,5,128,128]{3,2,1,0:T(8,128)} %param.58, f32[32,5,128,1]{2,1,0,3:T(8,128)S(1)} %multiply_bitcast_fusion.2), kind=kOutput, calls=%fused_computation.122 | convolution fusion | flops 31457280 | bytes 10584064 | tf_op jit(solution)/shard_map/bsij,bsj->bi/dot_general | solution.py:31
  359.6 42.1 %psum.121 = f32[3]{0:T(128)S(1)} all-reduce(f32[3]{0:T(128)S(1)} %convolution_bitcast_fusion.4), channel_id=1, replica_groups=mesh['dom'=32] {'dom'}, use_global_device_ids=true, to_apply=%region_18.0 | all-reduce | flops 3 | bytes 24 | tf_op jit(solution)/shard_map/psum | solution.py:62
  402.5 1.5 collective-permute-start.24
  406.2 2.5 collective-permute-done.26
  410.6 12.6 %fusion.24 = f32[32,1,128,1]{2,1,3,0:T(1,128)S(1)} fusion(f32[32,5,128,128]{3,2,1,0:T(8,128)} %param.58, f32[32,5,128,1]{2,1,0,3:T(8,128)S(1)} %multiply_bitcast_fusion.1), kind=kOutput, calls=%fused_computation.120 | convolution fusion | flops 31457280 | bytes 10584064 | tf_op jit(solution)/shard_map/bsij,bsj->bi/dot_general | solution.py:31
  424.2 42.2 %all-reduce.7 = (f32[]{:T(128)}, f32[3]{0:T(128)S(1)}, f32[]{:T(128)}) all-reduce(f32[]{:T(128)} %get-tuple-element.296, f32[3]{0:T(128)S(1)} %convolution_bitcast_fusion.3, f32[]{:T(128)} %get-tuple-element.295), channel_id=1, replica_groups=mesh['dom'=32] {'dom'}, use_global_device_ids=true, to_apply=%region_20.0 | all-reduce | flops 5 | bytes 40 | tf_op jit(solution)/shard_map/psum | solution.py:67
  472.4 1.5 collective-permute-done.30
  475.8 12.6 %fusion.22 = f32[32,1,128,1]{2,1,3,0:T(1,128)S(1)} fusion(f32[32,5,128,128]{3,2,1,0:T(8,128)} %param.58, f32[32,5,128,1]{2,1,0,3:T(8,128)S(1)} %multiply_bitcast_fusion), kind=kOutput, calls=%fused_computation.118 | convolution fusion | flops 31457280 | bytes 10584064 | tf_op jit(solution)/shard_map/bsij,bsj->bi/dot_general | solution.py:31
  489.5 42.7 %all-reduce.6 = (f32[]{:T(128)}, f32[3]{0:T(128)S(1)}, f32[]{:T(128)}) all-reduce(f32[]{:T(128)} %get-tuple-element.294, f32[3]{0:T(128)S(1)} %convolution_bitcast_fusion.2, f32[]{:T(128)} %get-tuple-element.293), channel_id=1, replica_groups=mesh['dom'=32] {'dom'}, use_global_device_ids=true, to_apply=%region_25.0 | all-reduce | flops 5 | bytes 40 | tf_op jit(solution)/shard_map/psum | solution.py:67
  533.8 2.5 fusion.77
  536.3 1.9 scatter.116
  (237 shorter events, 62.2 us)
Async XLA Ops:
  2.1 5.0 collective-permute-start
  3.6 3.6 collective-permute-start.1
  3.6 4.0 collective-permute-start.2
  4.1 4.5 collective-permute-start.3
  70.1 5.3 collective-permute-start.4
  74.1 1.4 collective-permute-start.5
  74.1 4.0 collective-permute-start.6
  74.6 4.5 collective-permute-start.7
  135.6 3.7 collective-permute-start.8
  137.1 2.2 collective-permute-start.9
  137.6 4.0 collective-permute-start.10
  138.1 4.5 collective-permute-start.11
  201.7 3.7 collective-permute-start.12
  203.1 2.4 collective-permute-start.13
  203.1 4.0 collective-permute-start.14
  203.6 4.5 collective-permute-start.15
  275.4 3.7 collective-permute-start.16
  276.7 2.4 collective-permute-start.17
  276.7 4.0 collective-permute-start.18
  277.2 4.5 collective-permute-start.19
  339.3 3.7 collective-permute-start.20
  340.7 2.4 collective-permute-start.21
  340.7 4.0 collective-permute-start.22
  341.2 4.5 collective-permute-start.23
  402.5 3.7 collective-permute-start.24
  404.6 1.6 collective-permute-start.25
  404.7 4.0 collective-permute-start.26
  405.2 4.5 collective-permute-start.27
  468.7 3.7 collective-permute-start.28
  470.0 2.4 collective-permute-start.29
  470.0 4.0 collective-permute-start.30
  470.5 4.5 collective-permute-start.31
  (2 other events, 44.2 us)
where the time goes:
time: 553 us; the launch traced here: 543 us
  blocking collectives  342 us (62%)
  matrix products  112 us (20%)
  waiting for transfers between devices  25.9 us (5%)
  starting transfers between devices  21.3 us (4%)
  local copies, waits for them, and re-layouts  17.9 us (3%)
  other arithmetic  16.4 us (3%)
  between operations  8.12 us (1%)
    psum x4, blocking collectives, krylov(): lax.psum((local_dots(vectors, mapped), jnp.sum(residue * mapped), jnp.sum...  170 us
    dot_general x8, matrix products, product(): jnp.einsum('bsij,bsj->bi', block_values, gathered, precision=lax.Precisio...  101 us
    psum x2, blocking collectives, krylov(): squared = lax.psum(jnp.sum(start * start), 'dom')  88.2 us
    psum x2, blocking collectives, krylov(): projection = lax.psum(local_dots(vectors, mapped), 'dom')  83.8 us
    ppermute x32, waiting for transfers between devices, passed_along(): lax.ppermute(value, axis, [(i, (i + by) % length) for i in range(length)])  25.9 us
    ppermute x32, starting transfers between devices, passed_along(): lax.ppermute(value, axis, [(i, (i + by) % length) for i in range(length)])  21.3 us
  transfers between devices with their start and end apart: 32, of which 22 were waited for; matrix products, arithmetic and copies ran while one was open for 1% of the time, Pallas kernels for 0%

commit v1 on v0

v1 whole, which is shorter than its diff:
```python
import functools

import jax
import jax.numpy as jnp
from jax import lax
from jax.experimental import pallas as pl
from jax.experimental.pallas import tpu as pltpu
from jax.sharding import PartitionSpec as P

KRYLOV = 3
RESTARTS = 2
OFFSETS = (-2, -1, 1, 2)
SHIFT = 8.0
SCALE = 4.0
GROUP = 8
EXCHANGES = 7
epsilon = 1e-06


def total(terms):
    result = terms[0]
    for term in terms[1:]:
        result = result + term
    return result


def quadratic(left, gram, right):
    return total(
        [a * total([gram[i][j] * b for j, b in enumerate(right)]) for i, a in enumerate(left)]
    )


def mapped_coefficients(c):
    result = [-SHIFT * c[0]]
    for i in range(1, len(c)):
        result.append(SCALE * c[i - 1] - SHIFT * c[i])
    result.append(SCALE * c[-1])
    return result


def subtract(a, weight, b):
    return [x - weight * b[i] if i < len(b) else x for i, x in enumerate(a)]


def multiply(a, b):
    size = len(a)
    result = []
    for i in range(size):
        row = []
        for j in range(size):
            terms = [
                a[i][k] * b[k][j]
                for k in range(size)
                if a[i][k] is not None and b[k][j] is not None
            ]
            row.append(total(terms) if terms else None)
        result.append(row)
    return result


def plus_identity(a, weight):
    return [
        [x * weight + 1.0 if i == j else x * weight for j, x in enumerate(row)]
        for i, row in enumerate(a)
    ]


def phi_column(hessenberg, substep):
    size = len(hessenberg)
    x = [
        [None if h is None else substep * h * (1.0 / 64.0) for h in row] for row in hessenberg
    ]
    one = jnp.ones_like(substep)
    zero = jnp.zeros_like(substep)
    series = [[one if i == j else zero for j in range(size)] for i in range(size)]
    for degree in range(12, 1, -1):
        series = plus_identity(multiply(x, series), 1.0 / degree)
    column = [series[i][0] * (1.0 / 64.0) for i in range(size)]
    power = plus_identity(multiply(x, series), 1.0)
    for turn in range(6):
        column = [
            total([power[i][k] * column[k] for k in range(size)]) + column[i] for i in range(size)
        ]
        if turn < 5:
            power = multiply(power, power)
    return column


def restart_coefficients(gram, substep):
    magnitude = jnp.sqrt(gram[0][0] + epsilon)
    basis = [[1.0 / magnitude]]
    hessenberg = [[None] * KRYLOV for _ in range(KRYLOV)]
    for column in range(KRYLOV):
        mapped = mapped_coefficients(basis[column])
        residue = mapped
        for k in range(column + 1):
            projection = quadratic(basis[k], gram, mapped)
            hessenberg[k][column] = projection
            residue = subtract(residue, projection, basis[k])
        if column + 1 < KRYLOV:
            squared = jnp.maximum(quadratic(residue, gram, residue), 0.0)
            length = jnp.sqrt(squared + epsilon)
            hessenberg[column + 1][column] = length
            inverse = 1.0 / length
            basis.append([x * inverse for x in residue])
    weights = phi_column(hessenberg, substep)
    factor = substep * magnitude
    return [
        factor * total([weights[k] * basis[k][i] for k in range(i, KRYLOV)]) for i in range(KRYLOV)
    ]


def kernel(n, *refs):
    (step_ref, columns_ref, lengths_ref, lists_ref, c_ref, r_ref, a_ref, y) = refs[:8]
    scratch = list(refs[8:])
    a, local, mixed = scratch[:3]
    extended = scratch[3 : 3 + EXCHANGES]
    packets = scratch[3 + EXCHANGES : 3 + 2 * EXCHANGES]
    rest = scratch[3 + 2 * EXCHANGES :]
    sums, partial = rest[:RESTARTS], rest[RESTARTS : 2 * RESTARTS]
    load_sem, send_sem, recv_sem, sum_send, sum_recv = rest[2 * RESTARTS :]

    bdev, width = c_ref.shape
    slots = columns_ref.shape[1]
    gmax = lists_ref.shape[1]
    blank = bdev + len(OFFSETS) * gmax
    groups = bdev // GROUP
    me = lax.axis_index("dom")

    loads = []
    for g in range(groups):
        rows = pl.ds(g * GROUP, GROUP)
        copy = pltpu.make_async_copy(a_ref.at[rows], a.at[rows], load_sem.at[g])
        copy.start()
        loads.append(copy)

    barrier = pltpu.get_barrier_semaphore()

    def greet(d, carry):
        pl.semaphore_signal(
            barrier,
            inc=1,
            device_id=(lax.rem(me + d, n),),
            device_id_type=pl.DeviceIdType.MESH,
        )
        return carry

    lax.fori_loop(1, n, greet, 0)

    def copies(e):
        return [
            pltpu.make_async_remote_copy(
                src_ref=packets[e].at[q],
                dst_ref=extended[e].at[pl.ds(bdev + q * gmax, gmax)],
                send_sem=send_sem.at[e, q],
                recv_sem=recv_sem.at[e, q],
                device_id=(lax.rem(me + offset + n, n),),
                device_id_type=pl.DeviceIdType.MESH,
            )
            for q, offset in enumerate(OFFSETS)
        ]

    def pack(e, field):
        local[...] = field
        extended[e][0:bdev, :] = field
        extended[e][blank:, :] = jnp.zeros((8, width), jnp.float32)
        for q in range(len(OFFSETS)):
            for g in range(gmax):
                packets[e][q, g : g + 1, :] = local[pl.ds(lists_ref[q, g], 1), :]

    def send(e):
        for copy in copies(e):
            copy.start()

    def arrive(e):
        for copy in copies(e):
            copy.wait_recv()

    row_of = lax.broadcasted_iota(jnp.int32, (GROUP, 2 * width), 0)

    def group_product(source, g):
        result = None
        for i in range(GROUP):
            row = g * GROUP + i
            length = lengths_ref[row]
            acc = None
            for t in range(slots):
                index = columns_ref[row, t]
                if t > 0:
                    index = jnp.where(t < length, index, blank)
                term = a[row, t] * source[pl.ds(index, 1), :]
                acc = term if acc is None else acc + term
            high = acc.astype(jnp.bfloat16)
            low = (acc - high.astype(jnp.float32)).astype(jnp.bfloat16)
            both = jnp.concatenate([high, low], axis=1)
            pick = jnp.where(row_of == i, 1.0, 0.0).astype(jnp.bfloat16)
            part = lax.dot_general(
                pick, both, (((1,), (1,)), ((), ())), preferred_element_type=jnp.float32
            )
            result = part if result is None else result + part
        return result

    def operator(source, first=False):
        def body(g, carry):
            if first:
                rows = pl.ds(pl.multiple_of(g * GROUP, GROUP), GROUP)
                pltpu.make_async_copy(a_ref.at[rows], a.at[rows], load_sem.at[g]).wait()
            y[pl.ds(pl.multiple_of(g * GROUP, GROUP), GROUP), :] = group_product(source, g)
            return carry

        lax.fori_loop(0, groups, body, 0)
        return y[...]

    lane = lax.broadcasted_iota(jnp.int32, (1, width), 1)

    def dots(fields):
        rows = jnp.zeros((1, width), jnp.float32)
        index = 0
        for i in range(len(fields)):
            for j in range(i, len(fields)):
                folded = jnp.sum(fields[i] * fields[j], axis=0, keepdims=True)
                value = jnp.sum(folded, axis=1, keepdims=True)
                rows = jnp.where(lane == index, value, rows)
                index += 1
        return rows

    def send_sums(turn, row):
        partial[turn][...] = row
        sums[turn][me] = row

        def one(d, carry):
            pltpu.make_async_remote_copy(
                src_ref=partial[turn],
                dst_ref=sums[turn].at[me],
                send_sem=sum_send.at[turn],
                recv_sem=sum_recv.at[turn],
                device_id=(lax.rem(me + d, n),),
                device_id_type=pl.DeviceIdType.MESH,
            ).start()
            return carry

        lax.fori_loop(1, n, one, 0)

    def gather_sums(turn, count):
        others = sums[turn].at[pl.ds(0, n - 1)]
        pltpu.make_async_copy(others, others, sum_recv.at[turn]).wait()
        row = jnp.sum(sums[turn][...], axis=0)
        gram = [[None] * count for _ in range(count)]
        index = 0
        for i in range(count):
            for j in range(i, count):
                value = jnp.sum(jnp.where(lane == index, row, 0.0), axis=1, keepdims=True)
                gram[i][j] = gram[j][i] = jnp.broadcast_to(value, (8, width))
                index += 1
        return gram

    def combine(weights, fields):
        return total(
            [
                jnp.concatenate([w] * (f.shape[0] // 8), axis=0) * f
                for w, f in zip(weights, fields)
            ]
        )

    concentration = c_ref[...]
    rate = r_ref[...]
    shifted = (rate * (1.0 - 2.0 * concentration) + SHIFT) * (1.0 / SCALE)
    substep = jnp.full((8, width), step_ref[0] * (1.0 / RESTARTS), jnp.float32)

    def apply(source, field):
        return shifted * field - operator(source) * (1.0 / SCALE)

    pack(0, concentration)
    pl.semaphore_wait(barrier, n - 1)
    send(0)
    arrive(0)
    field = rate * concentration * (1.0 - concentration) - operator(extended[0], first=True)

    fields = [field]
    for j in range(KRYLOV):
        pack(1 + j, field)
        send(1 + j)
        arrive(1 + j)
        field = apply(extended[1 + j], field)
        fields.append(field)

    pack(KRYLOV + 1, field)
    send_sums(0, dots(fields))
    send(KRYLOV + 1)
    d = restart_coefficients(gather_sums(0, KRYLOV + 1), substep)
    s = mapped_coefficients(d)
    s[0] = s[0] + 1.0
    start = combine(s, fields)
    arrive(KRYLOV + 1)
    mixed[0:bdev, :] = start
    mixed[bdev:blank, :] = combine(
        s, [extended[1 + j][bdev:blank, :] for j in range(KRYLOV + 1)]
    )
    mixed[blank:, :] = jnp.zeros((8, width), jnp.float32)
    base = concentration + combine(d, fields[:KRYLOV])

    field = apply(mixed, start)
    fields = [start, field]
    for j in range(1, KRYLOV):
        e = KRYLOV + 1 + j
        pack(e, field)
        send(e)
        arrive(e)
        field = apply(extended[e], field)
        fields.append(field)
    send_sums(1, dots(fields))
    d = restart_coefficients(gather_sums(1, KRYLOV + 1), substep)
    y[...] = base + combine(d, fields[:KRYLOV])

    for e in range(EXCHANGES):
        for copy in copies(e):
            copy.wait_send()
    for turn in range(RESTARTS):
        others = sums[turn].at[pl.ds(0, n - 1)]
        pltpu.make_async_copy(others, others, sum_send.at[turn]).wait()


def solution(mesh):
    n = mesh.shape["dom"]

    def shards(c, r, step, values, columns, lengths, lists):
        bdev, width = c.shape
        slots = columns.shape[1]
        sides, gmax = lists.shape[1:]
        tall = bdev + sides * gmax + 8
        f32 = jnp.float32
        smem = pl.BlockSpec(memory_space=pltpu.SMEM)
        vmem = pl.BlockSpec(memory_space=pltpu.VMEM)
        return pl.pallas_call(
            functools.partial(kernel, n),
            out_shape=jax.ShapeDtypeStruct((bdev, width), f32),
            in_specs=[smem] * 4 + [vmem] * 2 + [pl.BlockSpec(memory_space=pl.ANY)],
            out_specs=vmem,
            scratch_shapes=[
                pltpu.VMEM((bdev, slots, width, width), f32),
                pltpu.VMEM((bdev, width), f32),
                pltpu.VMEM((tall, width), f32),
            ]
            + [pltpu.VMEM((tall, width), f32)] * EXCHANGES
            + [pltpu.VMEM((sides, gmax, width), f32)] * EXCHANGES
            + [pltpu.VMEM((n, 1, width), f32)] * RESTARTS
            + [pltpu.VMEM((1, width), f32)] * RESTARTS
            + [
                pltpu.SemaphoreType.DMA((bdev // GROUP,)),
                pltpu.SemaphoreType.DMA((EXCHANGES, sides)),
                pltpu.SemaphoreType.DMA((EXCHANGES, sides)),
                pltpu.SemaphoreType.DMA((RESTARTS,)),
                pltpu.SemaphoreType.DMA((RESTARTS,)),
            ],
            compiler_params=pltpu.CompilerParams(
                collective_id=0, has_side_effects=True, vmem_limit_bytes=40 * 2**20
            ),
        )(step, columns, lengths, lists[0], c, r, values)

    placed = (
        P("dom", None),
        P("dom", None),
        P(),
        P("dom", None, None, None),
        P("dom", None),
        P("dom"),
        P("dom", None, None),
    )
    return jax.shard_map(
        shards, mesh=mesh, in_specs=placed, out_specs=P("dom", None), check_vma=False
    )
```

time: 553 us -> 64.9 us (0.12)
  the two profiles are of different devices: /device:TPU:12 before, /device:TPU:0 now
where the time goes in v1:
time: 64.9 us; the launch traced here: 64.5 us
  Pallas kernels  55.7 us (86%)
  local copies, waits for them, and re-layouts  8.12 us (13%)
  between operations  0.67 us (1%)
    pallas_call x1, Pallas kernels, shards(): pl.pallas_call(functools.partial(kernel, n), out_shape=jax.ShapeDtypeStru...  55.7 us
    unnamed x12, local copies, waits for them, and re-layouts  8.12 us

profile of v1, /device:TPU:0, one launch (start us, length us, event | category | flops | bytes accessed | tf_op | source)
XLA Modules:
  0.0 64.5 jit_solution(15082295398991198170)
XLA Ops:
  0.7 0.8 %copy.8.refs_1_ = s32[32,5]{1,0:T(8,128)S(1)} copy(s32[32,5]{0,1:T(8,128)} %param.11) | data formatting | bytes 1280 | tf_op args[4]
  1.4 0.0 copy-start
  1.4 4.0 %copy-done = f32[32,5,128,128]{3,2,1,0:T(8,128)S(1)} copy-done((f32[32,5,128,128]{3,2,1,0:T(8,128)S(1)}, f32[32,5,128,128]{3,2,1,0:T(8,128)}, u32[]{:S(2)}) %copy-start) | copy-done | bytes 10485784
  5.4 0.0 copy-start.1
  5.4 0.7 %copy-done.1 = f32[32,128]{1,0:T(8,128)S(1)} copy-done((f32[32,128]{1,0:T(8,128)S(1)}, f32[32,128]{1,0:T(8,128)}, u32[]{:S(2)}) %copy-start.1) | copy-done | bytes 16408
  6.1 0.0 copy-start.2
  6.1 0.7 %copy-done.2 = f32[32,128]{1,0:T(8,128)S(1)} copy-done((f32[32,128]{1,0:T(8,128)S(1)}, f32[32,128]{1,0:T(8,128)}, u32[]{:S(2)}) %copy-start.2) | copy-done | bytes 16408
  6.8 0.0 copy-start.3
  6.8 0.7 %copy-done.3 = s32[1,4,16]{2,1,0:T(4,128)S(1)} copy-done((s32[1,4,16]{2,1,0:T(4,128)S(1)}, s32[1,4,16]{2,1,0:T(4,128)}, u32[]{:S(2)}) %copy-start.3) | copy-done | bytes 280
  7.5 0.0 copy-start.4
  7.5 0.7 %copy-done.4 = s32[32]{0:T(128)S(1)} copy-done((s32[32]{0:T(128)S(1)}, s32[32]{0:T(128)}, u32[]{:S(2)}) %copy-start.4) | copy-done | bytes 152
  8.2 55.7 %shard_map.73 = f32[32,128]{1,0:T(8,128)S(1)} custom-call(f32[1]{0:T(128)S(6)} %copy.10.refs_0_, s32[32,5]{1,0:T(8,128)S(1)} %copy.8.refs_1_, s32[32]{0:T(128)S(1)} %copy-done.4, s32[4,16]{1,0:T(4,128)S(1)} %bitcast.1, f32[32,128]{1,0:T(8,128)S(1)} %copy-done.1, f32[32,128]{1,0:T(8,128)S(1)} %copy-done.2, f32[32,5,128,128]{3,2,1,0:T(8,128)S(1)} %copy-done), custom_call_target="tpu_custom_call" | custom-call | tf_op jit(solution)/shard_map/pallas_call | solution.py:334
  63.9 0.6 copy.11
Async XLA Ops:
  1.4 4.0 %copy-start = (f32[32,5,128,128]{3,2,1,0:T(8,128)S(1)}, f32[32,5,128,128]{3,2,1,0:T(8,128)}, u32[]{:S(2)}) copy-start(f32[32,5,128,128]{3,2,1,0:T(8,128)} %refs_6_.1) | copy-start | bytes 31457284
  5.4 0.7 %copy-start.1 = (f32[32,128]{1,0:T(8,128)S(1)}, f32[32,128]{1,0:T(8,128)}, u32[]{:S(2)}) copy-start(f32[32,128]{1,0:T(8,128)} %refs_4_.1) | copy-start | bytes 49156
  6.1 0.7 %copy-start.2 = (f32[32,128]{1,0:T(8,128)S(1)}, f32[32,128]{1,0:T(8,128)}, u32[]{:S(2)}) copy-start(f32[32,128]{1,0:T(8,128)} %refs_5_.1) | copy-start | bytes 49156
  6.8 0.7 %copy-start.3 = (s32[1,4,16]{2,1,0:T(4,128)S(1)}, s32[1,4,16]{2,1,0:T(4,128)}, u32[]{:S(2)}) copy-start(s32[1,4,16]{2,1,0:T(4,128)} %param.13) | copy-start | bytes 772
  7.5 0.7 %copy-start.4 = (s32[32]{0:T(128)S(1)}, s32[32]{0:T(128)}, u32[]{:S(2)}) copy-start(s32[32]{0:T(128)} %refs_2_.1) | copy-start | bytes 388

commit v2 on v1

--- a/solution.py
+++ b/solution.py
@@ -111,22 +111,30 @@
 
 
 def kernel(n, *refs):
-    (step_ref, columns_ref, lengths_ref, lists_ref, c_ref, r_ref, a_ref, y) = refs[:8]
-    scratch = list(refs[8:])
-    a, local, mixed = scratch[:3]
-    extended = scratch[3 : 3 + EXCHANGES]
-    packets = scratch[3 + EXCHANGES : 3 + 2 * EXCHANGES]
-    rest = scratch[3 + 2 * EXCHANGES :]
+    operands, a_ref, y = refs[:6], refs[6], refs[7]
+    staged = refs[8:14]
+    step_ref, columns_ref, lengths_ref, lists_ref, c_ref, r_ref = staged
+    scratch = list(refs[14:])
+    stage_sem, table, a, local, mixed = scratch[:5]
+    extended = scratch[5 : 5 + EXCHANGES]
+    packets = scratch[5 + EXCHANGES : 5 + 2 * EXCHANGES]
+    rest = scratch[5 + 2 * EXCHANGES :]
     sums, partial = rest[:RESTARTS], rest[RESTARTS : 2 * RESTARTS]
     load_sem, send_sem, recv_sem, sum_send, sum_recv = rest[2 * RESTARTS :]
 
     bdev, width = c_ref.shape
-    slots = columns_ref.shape[1]
+    slots = columns_ref.shape[0]
     gmax = lists_ref.shape[1]
     blank = bdev + len(OFFSETS) * gmax
     groups = bdev // GROUP
     me = lax.axis_index("dom")
 
+    stages = [
+        pltpu.make_async_copy(source, target, stage_sem.at[i])
+        for i, (source, target) in enumerate(zip(operands, staged))
+    ]
+    for copy in stages:
+        copy.start()
     loads = []
     for g in range(groups):
         rows = pl.ds(g * GROUP, GROUP)
@@ -146,6 +154,8 @@
         return carry
 
     lax.fori_loop(1, n, greet, 0)
+    for copy in stages:
+        copy.wait()
 
     def copies(e):
         return [
@@ -182,13 +192,9 @@
         result = None
         for i in range(GROUP):
             row = g * GROUP + i
-            length = lengths_ref[row]
             acc = None
             for t in range(slots):
-                index = columns_ref[row, t]
-                if t > 0:
-                    index = jnp.where(t < length, index, blank)
-                term = a[row, t] * source[pl.ds(index, 1), :]
+                term = a[row, t] * source[pl.ds(table[row * slots + t], 1), :]
                 acc = term if acc is None else acc + term
             high = acc.astype(jnp.bfloat16)
             low = (acc - high.astype(jnp.float32)).astype(jnp.bfloat16)
@@ -213,16 +219,12 @@
 
     lane = lax.broadcasted_iota(jnp.int32, (1, width), 1)
 
-    def dots(fields):
-        rows = jnp.zeros((1, width), jnp.float32)
-        index = 0
-        for i in range(len(fields)):
-            for j in range(i, len(fields)):
-                folded = jnp.sum(fields[i] * fields[j], axis=0, keepdims=True)
-                value = jnp.sum(folded, axis=1, keepdims=True)
-                rows = jnp.where(lane == index, value, rows)
-                index += 1
-        return rows
+    def dots(row, fields, last):
+        for i in range(last + 1):
+            folded = jnp.sum(fields[i] * fields[last], axis=0, keepdims=True)
+            value = jnp.sum(folded, axis=1, keepdims=True)
+            row = jnp.where(lane == last * (last + 1) // 2 + i, value, row)
+        return row
 
     def send_sums(turn, row):
         partial[turn][...] = row
@@ -246,12 +248,11 @@
         pltpu.make_async_copy(others, others, sum_recv.at[turn]).wait()
         row = jnp.sum(sums[turn][...], axis=0)
         gram = [[None] * count for _ in range(count)]
-        index = 0
-        for i in range(count):
-            for j in range(i, count):
+        for j in range(count):
+            for i in range(j + 1):
+                index = j * (j + 1) // 2 + i
                 value = jnp.sum(jnp.where(lane == index, row, 0.0), axis=1, keepdims=True)
                 gram[i][j] = gram[j][i] = jnp.broadcast_to(value, (8, width))
-                index += 1
         return gram
 
     def combine(weights, fields):
@@ -273,42 +274,63 @@
     pack(0, concentration)
     pl.semaphore_wait(barrier, n - 1)
     send(0)
+
+    def fill(row, carry):
+        length = lengths_ref[row]
+        for t in range(slots):
+            table[row * slots + t] = jnp.where(t < length, columns_ref[t, row], blank)
+        return carry
+
+    lax.fori_loop(0, bdev, fill, 0)
     arrive(0)
     field = rate * concentration * (1.0 - concentration) - operator(extended[0], first=True)
 
     fields = [field]
+    row = jnp.zeros((1, width), jnp.float32)
     for j in range(KRYLOV):
         pack(1 + j, field)
         send(1 + j)
+        row = dots(row, fields, j)
         arrive(1 + j)
         field = apply(extended[1 + j], field)
         fields.append(field)
 
-    pack(KRYLOV + 1, field)
-    send_sums(0, dots(fields))
-    send(KRYLOV + 1)
+    e = KRYLOV + 1
+    pack(e, field)
+    send(e)
+    send_sums(0, dots(row, fields, KRYLOV))
+    arrive(e)
+    field = apply(extended[e], field)
+    fields.append(field)
+    e = KRYLOV + 2
+    pack(e, field)
+    send(e)
     d = restart_coefficients(gather_sums(0, KRYLOV + 1), substep)
     s = mapped_coefficients(d)
     s[0] = s[0] + 1.0
-    start = combine(s, fields)
-    arrive(KRYLOV + 1)
-    mixed[0:bdev, :] = start
+    start = combine(s, fields[:-1])
+    field = combine(s, fields[1:])
+    base = concentration + combine(d, fields[:KRYLOV])
+    mixed[0:bdev, :] = field
+    mixed[blank:, :] = jnp.zeros((8, width), jnp.float32)
+    fields = [start, field]
+    row = jnp.zeros((1, width), jnp.float32)
+    row = dots(dots(row, fields, 0), fields, 1)
+    arrive(e)
     mixed[bdev:blank, :] = combine(
-        s, [extended[1 + j][bdev:blank, :] for j in range(KRYLOV + 1)]
+        s, [extended[2 + j][bdev:blank, :] for j in range(KRYLOV + 1)]
     )
-    mixed[blank:, :] = jnp.zeros((8, width), jnp.float32)
-    base = concentration + combine(d, fields[:KRYLOV])
-
-    field = apply(mixed, start)
-    fields = [start, field]
-    for j in range(1, KRYLOV):
+    field = apply(mixed, field)
+    fields.append(field)
+    for j in range(2, KRYLOV):
         e = KRYLOV + 1 + j
         pack(e, field)
         send(e)
+        row = dots(row, fields, j)
         arrive(e)
         field = apply(extended[e], field)
         fields.append(field)
-    send_sums(1, dots(fields))
+    send_sums(1, dots(row, fields, KRYLOV))
     d = restart_coefficients(gather_sums(1, KRYLOV + 1), substep)
     y[...] = base + combine(d, fields[:KRYLOV])
 
@@ -329,14 +351,22 @@
         sides, gmax = lists.shape[1:]
         tall = bdev + sides * gmax + 8
         f32 = jnp.float32
-        smem = pl.BlockSpec(memory_space=pltpu.SMEM)
+        held = pl.BlockSpec(memory_space=pltpu.HBM)
         vmem = pl.BlockSpec(memory_space=pltpu.VMEM)
         return pl.pallas_call(
             functools.partial(kernel, n),
             out_shape=jax.ShapeDtypeStruct((bdev, width), f32),
-            in_specs=[smem] * 4 + [vmem] * 2 + [pl.BlockSpec(memory_space=pl.ANY)],
+            in_specs=[held] * 7,
             out_specs=vmem,
             scratch_shapes=[
+                pltpu.SMEM((1,), f32),
+                pltpu.SMEM((slots, bdev), jnp.int32),
+                pltpu.SMEM((bdev,), jnp.int32),
+                pltpu.SMEM((sides, gmax), jnp.int32),
+                pltpu.VMEM((bdev, width), f32),
+                pltpu.VMEM((bdev, width), f32),
+                pltpu.SemaphoreType.DMA((6,)),
+                pltpu.SMEM((bdev * slots,), jnp.int32),
                 pltpu.VMEM((bdev, slots, width, width), f32),
                 pltpu.VMEM((bdev, width), f32),
                 pltpu.VMEM((tall, width), f32),
@@ -353,9 +383,9 @@
                 pltpu.SemaphoreType.DMA((RESTARTS,)),
             ],
             compiler_params=pltpu.CompilerParams(
-                collective_id=0, has_side_effects=True, vmem_limit_bytes=40 * 2**20
+                collective_id=0, has_side_effects=True, vmem_limit_bytes=67043328
             ),
-        )(step, columns, lengths, lists[0], c, r, values)
+        )(step, columns.T, lengths, lists[0], c, r, values)
 
     placed = (
         P("dom", None),

time: 64.9 us -> 56.4 us (0.87)
  local copies, waits for them, and re-layouts: 8.12 us -> 1.32 us
  Pallas kernels: 55.7 us -> 54.2 us
    unnamed x12 -> x1, local copies, waits for them, and re-layouts: 8.12 us -> 1.32 us
    pallas_call x1, Pallas kernels: 55.7 us -> 54.2 us  [shards(): pl.pallas_call(functools.partial(kernel, n), out_shape=jax.ShapeDtypeStru...]
where the time goes in v2:
time: 56.4 us; the launch traced here: 56.1 us
  Pallas kernels  54.2 us (96%)
  local copies, waits for them, and re-layouts  1.32 us (2%)
  between operations  0.66 us (1%)
    pallas_call x1, Pallas kernels, shards(): pl.pallas_call(functools.partial(kernel, n), out_shape=jax.ShapeDtypeStru...  54.2 us
    unnamed x1, local copies, waits for them, and re-layouts  1.32 us

profile of v2, /device:TPU:0, one launch (start us, length us, event | category | flops | bytes accessed | tf_op | source)
XLA Modules:
  0.0 56.1 jit_solution(5373770197529555865)
XLA Ops:
  0.7 54.2 %shard_map.73 = f32[32,128]{1,0:T(8,128)} custom-call(f32[1]{0:T(128)S(6)} %copy.9.refs_0_, s32[5,32]{1,0:T(8,128)} %bitcast.2, s32[32]{0:T(128)} %refs_2_.1, s32[4,16]{1,0:T(4,128)} %bitcast.3, f32[32,128]{1,0:T(8,128)} %refs_4_.1, f32[32,128]{1,0:T(8,128)} %refs_5_.1, f32[32,5,128,128]{3,2,1,0:T(8,128)} %refs_6_.1), custom_call_target="tpu_custom_call" | custom-call | tf_op jit(solution)/shard_map/pallas_call | solution.py:356
  54.8 1.3 %copy.10 = f32[32,128]{1,0:T(8,128)} copy(f32[32,128]{1,0:T(8,128)} %shard_map.73) | data formatting | bytes 32768

commit v3 on v2

--- a/solution.py
+++ b/solution.py
@@ -172,8 +172,6 @@
 
     def pack(e, field):
         local[...] = field
-        extended[e][0:bdev, :] = field
-        extended[e][blank:, :] = jnp.zeros((8, width), jnp.float32)
         for q in range(len(OFFSETS)):
             for g in range(gmax):
                 packets[e][q, g : g + 1, :] = local[pl.ds(lists_ref[q, g], 1), :]
@@ -181,6 +179,8 @@
     def send(e):
         for copy in copies(e):
             copy.start()
+        extended[e][0:bdev, :] = local[...]
+        extended[e][blank:, :] = jnp.zeros((8, width), jnp.float32)
 
     def arrive(e):
         for copy in copies(e):
@@ -206,16 +206,8 @@
             result = part if result is None else result + part
         return result
 
-    def operator(source, first=False):
-        def body(g, carry):
-            if first:
-                rows = pl.ds(pl.multiple_of(g * GROUP, GROUP), GROUP)
-                pltpu.make_async_copy(a_ref.at[rows], a.at[rows], load_sem.at[g]).wait()
-            y[pl.ds(pl.multiple_of(g * GROUP, GROUP), GROUP), :] = group_product(source, g)
-            return carry
-
-        lax.fori_loop(0, groups, body, 0)
-        return y[...]
+    def operator(source):
+        return jnp.concatenate([group_product(source, g) for g in range(groups)], axis=0)
 
     lane = lax.broadcasted_iota(jnp.int32, (1, width), 1)
 
@@ -282,8 +274,10 @@
         return carry
 
     lax.fori_loop(0, bdev, fill, 0)
+    for copy in loads:
+        copy.wait()
     arrive(0)
-    field = rate * concentration * (1.0 - concentration) - operator(extended[0], first=True)
+    field = rate * concentration * (1.0 - concentration) - operator(extended[0])
 
     fields = [field]
     row = jnp.zeros((1, width), jnp.float32)

time: 56.4 us -> 53.7 us (0.952)
  Pallas kernels: 54.2 us -> 51.4 us
    pallas_call x1, Pallas kernels: 54.2 us -> 51.4 us  [shards(): pl.pallas_call(functools.partial(kernel, n), out_shape=jax.ShapeDtypeStru...]
where the time goes in v3:
time: 53.7 us; the launch traced here: 53.4 us
  Pallas kernels  51.4 us (96%)
  local copies, waits for them, and re-layouts  1.32 us (2%)
  between operations  0.66 us (1%)
    pallas_call x1, Pallas kernels, shards(): pl.pallas_call(functools.partial(kernel, n), out_shape=jax.ShapeDtypeStru...  51.4 us
    unnamed x1, local copies, waits for them, and re-layouts  1.32 us

profile of v3, /device:TPU:0, one launch (start us, length us, event | category | flops | bytes accessed | tf_op | source)
XLA Modules:
  0.0 53.4 jit_solution(7056533401934156488)
XLA Ops:
  0.7 51.4 %shard_map.73 = f32[32,128]{1,0:T(8,128)} custom-call(f32[1]{0:T(128)S(6)} %copy.9.refs_0_, s32[5,32]{1,0:T(8,128)} %bitcast.2, s32[32]{0:T(128)} %refs_2_.1, s32[4,16]{1,0:T(4,128)} %bitcast.3, f32[32,128]{1,0:T(8,128)} %refs_4_.1, f32[32,128]{1,0:T(8,128)} %refs_5_.1, f32[32,5,128,128]{3,2,1,0:T(8,128)} %refs_6_.1), custom_call_target="tpu_custom_call" | custom-call | tf_op jit(solution)/shard_map/pallas_call | solution.py:350
  52.1 1.3 %copy.10 = f32[32,128]{1,0:T(8,128)} copy(f32[32,128]{1,0:T(8,128)} %shard_map.73) | data formatting | bytes 32768
